TPU v7x, 32 devices: a whole 2x2x4 slice. The times are simulated.
32 devices in a mesh: dp: 4 (over x, core), mp: 8 (over z, y).
Axes of the slice: x: 2, y: 2, z: 4, core: 2. Of those that a mesh axis runs over, the one named last changes fastest.
Arguments:
- cotangent: bfloat16 [512, 4608], P(('dp', 'mp')), may hold values from -50 to 50
- mlp_out: bfloat16 [512, 4608], P(('dp', 'mp')), may hold values from -500 to 500
- post_gain: float32 [4608], replicated, may hold values from 0.5 to 1.5
- down_weight: bfloat16 [36864, 4608], P('mp', 'dp'), may hold values from -0.09375 to 0.09375
- gate_pre: bfloat16 [512, 36864], P('dp', 'mp'), may hold values from -6 to 6
- up_pre: bfloat16 [512, 36864], P('dp', 'mp'), may hold values from -6 to 6
Outputs:
- gate_grad: float32 [512, 36864], P('dp', 'mp')
- up_grad: float32 [512, 36864], P('dp', 'mp')
- gain_grad: float32 [4608], replicated
All inputs are finite; a program needn't handle non-finite values.
Results may differ from a plain program's by a relative error of at most 0.0005.
Values may be sent and summed in bfloat16 or wider, within the bound.
A program may use at most 64 MiB of HBM per device.

v0:
```python
import jax
import jax.numpy as jnp
from jax import lax
from jax.sharding import PartitionSpec as P

D = 4608
epsilon = 1e-06


def gelu_tanh(values):
    return jax.nn.gelu(values, approximate=True)


def local(cotangent, mlp_out, post_gain, down_weight, gate_pre, up_pre):
    forward = mlp_out.astype(jnp.float32)
    upstream = cotangent.astype(jnp.float32)
    root_mean = jnp.sqrt(jnp.mean(forward * forward, axis=1, keepdims=True) + epsilon)
    normed = forward / root_mean
    gain_part = jnp.sum(upstream * normed, axis=0)
    scaled = upstream * post_gain[None, :]
    project_sum = jnp.sum(scaled * forward, axis=1, keepdims=True)
    out_grad = scaled / root_mean - forward * project_sum / (D * root_mean**3)
    hid_units = down_weight.shape[0]
    gain_grad = lax.psum(gain_part, ("dp", "mp"))
    pieces = lax.all_to_all(out_grad, "dp", split_axis=1, concat_axis=0, tiled=True)
    weight_local = down_weight.astype(jnp.float32)
    partial_value = jnp.dot(
        lax.all_gather(pieces, "mp", axis=0, tiled=True),
        weight_local.T,
        precision=lax.Precision.HIGHEST,
    )
    dp_count = lax.axis_size("dp")
    mp_count = lax.axis_size("mp")
    row_count = out_grad.shape[0]
    partial_value = partial_value.reshape(mp_count, dp_count * row_count, hid_units)
    summed = lax.psum_scatter(partial_value, "dp", scatter_dimension=1, tiled=True)
    hidden_grad = summed.reshape(mp_count * row_count, hid_units)
    gate_val = gate_pre.astype(jnp.float32)
    up_val = up_pre.astype(jnp.float32)
    act_val, pull_back = jax.vjp(gelu_tanh, gate_val)
    gate_grad = pull_back(hidden_grad * up_val)[0]
    up_grad = hidden_grad * act_val
    return (gate_grad, up_grad, gain_grad)


def solution(mesh):
    return jax.shard_map(
        local,
        mesh=mesh,
        in_specs=(
            P(("dp", "mp"), None),
            P(("dp", "mp"), None),
            P(),
            P("mp", "dp"),
            P("dp", "mp"),
            P("dp", "mp"),
        ),
        out_specs=(P("dp", "mp"), P("dp", "mp"), P()),
        check_vma=False,
    )
```

profile of v0, /device:TPU:0, one launch (start us, length us, event | category | flops | bytes accessed | tf_op | source)
XLA Modules:
  0.0 187.1 jit_solution(5941770654814540855)
XLA Ops:
  7.2 0.0 all-gather.2.cloned.1.call-start
  7.2 1.1 fusion.12
  8.3 1.3 fusion.11
  9.5 1.1 fusion.10
  10.7 10.5 %all_to_all.19 = f32[16,4,1152]{2,0,1:T(8,128)} all-to-all(f32[16,4,1152]{2,0,1:T(8,128)S(1)} %bitcast.17), channel_id=1, replica_groups=mesh['dp'=4,'mp'=8] {'dp'}, dimensions={1} | all-to-all | bytes 589824 | tf_op jit(solution)/shard_map/all_to_all | solution.py:25
  21.2 0.0 all-gather.2.cloned.1.call-update
  21.2 0.0 reduce-scatter.2.cloned.1.call-start
  21.3 52.6 %all-gather.2.cloned.1.call-done = f32[512,1152]{1,0:T(8,128)} async-done(((f32[64,1152]{1,0:T(8,128)}), f32[512,1152]{1,0:T(8,128)}) %all-gather.2.cloned.1.call-update) | async-done | bytes 2359312 | tf_op jit(solution)/shard_map/all_gather | solution.py:28
  73.9 23.4 %fusion.16 = f32[512,4608]{1,0:T(8,128)} fusion(f32[512,1152]{1,0:T(8,128)} %all-gather.2.cloned.1.call-done, bf16[4608,1152]{1,0:T(8,128)(2,1)} %param.9), kind=kOutput, calls=%fused_computation.31 | convolution fusion | flops 32614907904 | bytes 22413312 | tf_op jit(solution)/shard_map/dot_general | solution.py:27
  97.2 0.0 copy-start
  97.2 0.0 copy-start.1
  97.3 0.0 reduce-scatter.2.cloned.1.call-update
  97.3 40.2 %psum.7 = f32[4608]{0:T(1024)} all-reduce(f32[4608]{0:T(1024)S(1)} %get-tuple-element.3), channel_id=1, replica_groups=mesh['dp'=4,'mp'=8] {'dp','mp'}, use_global_device_ids=true, to_apply=%region_4.0 | all-reduce | flops 4608 | bytes 36864 | tf_op jit(solution)/shard_map/psum | solution.py:24
  137.5 37.0 %reduce-scatter.2.cloned.1.call-done = f32[8,16,4608]{2,1,0:T(8,128)} async-done(((f32[8,64,4608]{2,1,0:T(8,128)}), f32[8,16,4608]{2,1,0:T(8,128)}) %reduce-scatter.2.cloned.1.call-update) | async-done | bytes 2359312 | tf_op jit(solution)/shard_map/reduce_scatter | solution.py:36
  174.5 0.0 copy-done
  174.5 0.0 copy-done.1
  174.5 5.8 %fusion.8 = (f32[128,4608]{1,0:T(8,128)}, f32[128,4608]{1,0:T(8,128)}) fusion(bf16[128,4608]{1,0:T(8,128)(2,1)S(1)} %copy-done, f32[8,16,4608]{2,1,0:T(8,128)} %reduce-scatter.2.cloned.1.call-done, bf16[128,4608]{1,0:T(8,128)(2,1)S(1)} %copy-done.1), kind=kLoop, calls=%fused_computation.13 | loop fusion | flops 14155776 | bytes 9437184 | tf_op jit(solution)/shard_map/mul | solution.py:42
  (2 shorter events, 0.0 us)
Async XLA Ops:
  7.2 66.7 %all-gather.2.cloned.1.call-start = ((), (), s32[]{:S(2)}) async-start(), calls=%async_computation.2 | async-start | bytes 2654208 | tf_op jit(solution)/shard_map/all_gather | solution.py:28
  21.2 153.3 %reduce-scatter.2.cloned.1.call-start = ((), (), s32[]{:S(2)}) async-start(), calls=%async_computation.3 | async-start | bytes 11796480 | tf_op jit(solution)/shard_map/reduce_scatter | solution.py:36
  97.2 77.3 %copy-start = (bf16[128,4608]{1,0:T(8,128)(2,1)S(1)}, bf16[128,4608]{1,0:T(8,128)(2,1)}, u32[]{:S(2)}) copy-start(bf16[128,4608]{1,0:T(8,128)(2,1)} %param.10) | copy-start | bytes 3538948
  97.2 77.3 %copy-start.1 = (bf16[128,4608]{1,0:T(8,128)(2,1)S(1)}, bf16[128,4608]{1,0:T(8,128)(2,1)}, u32[]{:S(2)}) copy-start(bf16[128,4608]{1,0:T(8,128)(2,1)} %param.11) | copy-start | bytes 3538948
Sparse Core Ops, SparseCore 0:
  21.3 52.5 all-gather.1
  97.4 77.0 reduce-scatter.1
where the time goes:
time: 187 us
  waiting for transfers between devices  89.7 us (48%)
  blocking collectives  50.7 us (27%)
  matrix products  23.4 us (13%)
  between operations  14.1 us (8%)
  other arithmetic  9.22 us (5%)
    all_gather x1, waiting for transfers between devices, local(): lax.all_gather(pieces, 'mp', axis=0, tiled=True)  52.6 us
    psum x1, blocking collectives, local(): gain_grad = lax.psum(gain_part, ('dp', 'mp'))  40.2 us
    reduce_scatter x1, waiting for transfers between devices, local(): lax.psum_scatter(partial_value, 'dp', scatter_dimension=1, tiled=True)  37 us
    dot_general x1, matrix products, local(): jnp.dot(lax.all_gather(pieces, 'mp', axis=0, tiled=True), weight_local.T,...  23.4 us
    all_to_all x1, blocking collectives, local(): lax.all_to_all(out_grad, 'dp', split_axis=1, concat_axis=0, tiled=True)  10.5 us
    mul x1, other arithmetic, local(): up_grad = hidden_grad * act_val  5.78 us
  transfers between devices with their start and end apart: 2, of which 2 were waited for; matrix products, arithmetic and copies ran while one was open for 0% of the time, Pallas kernels for 0%

commit v1 on v0

--- a/solution.py
+++ b/solution.py
@@ -22,7 +22,10 @@
     out_grad = scaled / root_mean - forward * project_sum / (D * root_mean**3)
     hid_units = down_weight.shape[0]
     gain_grad = lax.psum(gain_part, ("dp", "mp"))
-    pieces = lax.all_to_all(out_grad, "dp", split_axis=1, concat_axis=0, tiled=True)
+    pieces = jnp.concatenate(
+        lax.all_to_all(jnp.stack(jnp.split(out_grad, lax.axis_size("dp"), axis=1)), "dp", 0, 0),
+        axis=0,
+    )
     weight_local = down_weight.astype(jnp.float32)
     partial_value = jnp.dot(
         lax.all_gather(pieces, "mp", axis=0, tiled=True),

time: 187 us -> 187 us (level)
  no operation moved by 1% of the time
where the time goes in v1:
time: 187 us
  waiting for transfers between devices  89.7 us (48%)
  blocking collectives  50.7 us (27%)
  matrix products  23.4 us (13%)
  between operations  14.1 us (8%)
  other arithmetic  9.24 us (5%)
    all_gather x1, waiting for transfers between devices, local(): lax.all_gather(pieces, 'mp', axis=0, tiled=True)  52.6 us
    psum x1, blocking collectives, local(): gain_grad = lax.psum(gain_part, ('dp', 'mp'))  40.2 us
    reduce_scatter x1, waiting for transfers between devices, local(): lax.psum_scatter(partial_value, 'dp', scatter_dimension=1, tiled=True)  37 us
    dot_general x1, matrix products, local(): jnp.dot(lax.all_gather(pieces, 'mp', axis=0, tiled=True), weight_local.T,...  23.4 us
    all_to_all x1, blocking collectives, local(): lax.all_to_all(jnp.stack(jnp.split(out_grad, lax.axis_size('dp'), axis=1)...  10.5 us
    mul x1, other arithmetic, local(): up_grad = hidden_grad * act_val  5.78 us
  transfers between devices with their start and end apart: 2, of which 2 were waited for; matrix products, arithmetic and copies ran while one was open for 0% of the time, Pallas kernels for 0%

profile of v1, /device:TPU:0, one launch (start us, length us, event | category | flops | bytes accessed | tf_op | source)
XLA Modules:
  0.0 187.2 jit_solution(6773080797404878615)
XLA Ops:
  7.2 0.0 all-gather.2.cloned.1.call-start
  7.2 1.1 fusion.12
  8.3 1.3 fusion.11
  9.5 1.1 fusion.10
  10.7 10.5 %all_to_all.5 = f32[4,16,1152]{2,1,0:T(8,128)} all-to-all(f32[4,16,1152]{2,1,0:T(8,128)S(1)} %pad_maximum_fusion), channel_id=1, replica_groups=mesh['dp'=4,'mp'=8] {'dp'}, dimensions={0} | all-to-all | bytes 589824 | tf_op jit(solution)/shard_map/all_to_all | solution.py:26
  21.2 0.0 all-gather.2.cloned.1.call-update
  21.2 0.0 reduce-scatter.2.cloned.1.call-start
  21.3 52.6 %all-gather.2.cloned.1.call-done = f32[512,1152]{1,0:T(8,128)} async-done(((f32[64,1152]{1,0:T(8,128)}), f32[512,1152]{1,0:T(8,128)}) %all-gather.2.cloned.1.call-update) | async-done | bytes 2359312 | tf_op jit(solution)/shard_map/all_gather | solution.py:31
  73.9 23.4 %fusion.16 = f32[512,4608]{1,0:T(8,128)} fusion(f32[512,1152]{1,0:T(8,128)} %all-gather.2.cloned.1.call-done, bf16[4608,1152]{1,0:T(8,128)(2,1)} %param.9), kind=kOutput, calls=%fused_computation.35 | convolution fusion | flops 32614907904 | bytes 22413312 | tf_op jit(solution)/shard_map/dot_general | solution.py:30
  97.3 0.0 copy-start
  97.3 0.0 copy-start.1
  97.3 0.0 reduce-scatter.2.cloned.1.call-update
  97.3 40.2 %psum.7 = f32[4608]{0:T(1024)} all-reduce(f32[4608]{0:T(1024)S(1)} %get-tuple-element.3), channel_id=1, replica_groups=mesh['dp'=4,'mp'=8] {'dp','mp'}, use_global_device_ids=true, to_apply=%region_4.0 | all-reduce | flops 4608 | bytes 36864 | tf_op jit(solution)/shard_map/psum | solution.py:24
  137.5 37.0 %reduce-scatter.2.cloned.1.call-done = f32[8,16,4608]{2,1,0:T(8,128)} async-done(((f32[8,64,4608]{2,1,0:T(8,128)}), f32[8,16,4608]{2,1,0:T(8,128)}) %reduce-scatter.2.cloned.1.call-update) | async-done | bytes 2359312 | tf_op jit(solution)/shard_map/reduce_scatter | solution.py:39
  174.5 0.0 copy-done
  174.5 0.0 copy-done.1
  174.5 5.8 %fusion.8 = (f32[128,4608]{1,0:T(8,128)}, f32[128,4608]{1,0:T(8,128)}) fusion(bf16[128,4608]{1,0:T(8,128)(2,1)S(1)} %copy-done, f32[8,16,4608]{2,1,0:T(8,128)} %reduce-scatter.2.cloned.1.call-done, bf16[128,4608]{1,0:T(8,128)(2,1)S(1)} %copy-done.1), kind=kLoop, calls=%fused_computation.13 | loop fusion | flops 14155776 | bytes 9437184 | tf_op jit(solution)/shard_map/mul | solution.py:45
  (3 shorter events, 0.1 us)
Async XLA Ops:
  7.2 66.8 %all-gather.2.cloned.1.call-start = ((), (), s32[]{:S(2)}) async-start(), calls=%async_computation.2 | async-start | bytes 2654208 | tf_op jit(solution)/shard_map/all_gather | solution.py:31
  21.2 153.3 %reduce-scatter.2.cloned.1.call-start = ((), (), s32[]{:S(2)}) async-start(), calls=%async_computation.3 | async-start | bytes 11796480 | tf_op jit(solution)/shard_map/reduce_scatter | solution.py:39
  97.3 77.3 %copy-start = (bf16[128,4608]{1,0:T(8,128)(2,1)S(1)}, bf16[128,4608]{1,0:T(8,128)(2,1)}, u32[]{:S(2)}) copy-start(bf16[128,4608]{1,0:T(8,128)(2,1)} %param.10) | copy-start | bytes 3538948
  97.3 77.3 %copy-start.1 = (bf16[128,4608]{1,0:T(8,128)(2,1)S(1)}, bf16[128,4608]{1,0:T(8,128)(2,1)}, u32[]{:S(2)}) copy-start(bf16[128,4608]{1,0:T(8,128)(2,1)} %param.11) | copy-start | bytes 3538948
Sparse Core Ops, SparseCore 0:
  21.4 52.5 all-gather.1
  97.4 77.0 reduce-scatter.1
